TPU v7x, 128 devices: a whole 4x4x4 slice. The times are simulated.
128 devices in a mesh: fsdp: 32 (over z, y, x_hi), sp: 4 (over x_lo, core).
Axes of the slice: x: 4 (x_hi: 2, x_lo: 2; x = x_hi * 2 + x_lo), y: 4, z: 4, core: 2. Of those that a mesh axis runs over, the one named last changes fastest.
Arguments:
- tokens: bfloat16 [32, 512, 1536], P('fsdp', 'sp'), may hold values from -6 to 6
- modulation: float32 [32, 1, 6, 1536], P('fsdp'), may hold values from -4 to 4
- w_qkv: bfloat16 [1, 1536, 3, 1536], P(None, 'fsdp', None, 'sp'), may hold values from -0.15625 to 0.15625
- w_out: bfloat16 [1, 1536, 1536], P(None, 'sp', 'fsdp'), may hold values from -0.15625 to 0.15625
- w_in: bfloat16 [1, 1536, 6144], P(None, 'fsdp', 'sp'), may hold values from -0.15625 to 0.15625
- w_back: bfloat16 [1, 6144, 1536], P(None, 'sp', 'fsdp'), may hold values from -0.078125 to 0.078125
- out_grad: bfloat16 [32, 512, 1536], P('fsdp', 'sp'), may hold values from -6 to 6
Outputs:
- final_out: bfloat16 [32, 512, 1536], P('fsdp', 'sp')
- input_grad: float32 [32, 512, 1536], P('fsdp', 'sp')
- grad_qkv: float32 [1, 1536, 3, 1536], P(None, 'fsdp', None, 'sp')
- grad_out: float32 [1, 1536, 1536], P(None, 'sp', 'fsdp')
- grad_in: float32 [1, 1536, 6144], P(None, 'fsdp', 'sp')
- grad_back: float32 [1, 6144, 1536], P(None, 'sp', 'fsdp')
All inputs are finite; a program needn't handle non-finite values.
Results may differ from a plain program's by a relative error of at most 0.03.
Values may be sent and summed in bfloat16 or wider, within the bound.
No kernel may reach another device: no remote copies, remote signals or barrier semaphores. Data moves between devices by JAX's collectives and lax.ppermute only.
A program may use at most 128 MiB of HBM per device.

v0:
```python
import math

import jax
import jax.numpy as jnp
from jax import lax
from jax.sharding import Mesh
from jax.sharding import PartitionSpec as P

HEAD_DIM = 128
SP = ("sp_0", "sp_1")


ln_eps = 1e-06
temper = 2.5
block_limit = 512


def laid_out(blocks, dim):
    blocks = jnp.moveaxis(blocks, 0, dim)
    lengths = blocks.shape
    return blocks.reshape(*lengths[:dim], lengths[dim] * lengths[dim + 1], *lengths[dim + 2 :])


def one_gather(arrays, axis, dims):
    ravelled = jnp.concatenate([a.reshape(-1) for a in arrays])
    lines, at, gathered = lax.all_gather(ravelled, axis), 0, []
    for a, dim in zip(arrays, dims):
        blocks = lines[:, at : at + a.size].reshape(-1, *a.shape)
        gathered.append(laid_out(blocks, dim))
        at += a.size
    return tuple(gathered)


def own_block(blocks, axes, turns):
    inside = blocks.shape[1:]
    blocks = blocks.reshape(*(lax.axis_size(a) for a in axes), *inside)
    blocks = jnp.moveaxis(blocks, turns, range(len(axes))).reshape(-1, *inside)
    for k in turns:
        blocks = lax.psum_scatter(blocks, axes[k], scatter_dimension=0, tiled=True)
    return blocks[0]


def cut_along(value, dim, count):
    return jnp.stack(jnp.split(value, count, axis=dim))


def sum_by_axis(value, axes, turns, dim):
    count = lax.axis_size(axes)
    return own_block(cut_along(value, dim, count), axes, turns)


def sum_packed(arrays, axis, dims):
    count = lax.axis_size(axis)
    blocks = [cut_along(a, dim, count) for a, dim in zip(arrays, dims)]
    lines = jnp.concatenate([b.reshape(count, -1) for b in blocks], axis=1)
    ravelled, at, gathered = lax.psum_scatter(lines, axis, tiled=True)[0], 0, []
    for b in blocks:
        part = b[0]
        gathered.append(ravelled[at : at + part.size].reshape(part.shape))
        at += part.size
    return tuple(gathered)


def normalize(stream):
    mean_part = jnp.mean(stream, axis=-1, keepdims=True)
    centred = stream - mean_part
    rstd = lax.rsqrt(jnp.mean(centred * centred, axis=-1, keepdims=True) + ln_eps)
    return (centred * rstd, rstd)


def norm_back(normed, rstd, incoming):
    first = jnp.mean(incoming, axis=-1, keepdims=True)
    second = jnp.mean(incoming * normed, axis=-1, keepdims=True)
    return rstd * (incoming - first - normed * second)


def gelu_tanh(hidden):
    return jax.nn.gelu(hidden, approximate=True)


def project(left, weight):
    flat_rows = left.reshape(-1, left.shape[-1])
    result = jnp.dot(flat_rows, weight, preferred_element_type=jnp.float32)
    return result.reshape(left.shape[:-1] + (weight.shape[1],))


def project_back(left, weight):
    flat_rows = left.reshape(-1, left.shape[-1])
    result = lax.dot_general(
        flat_rows, weight, (((1,), (1,)), ((), ())), preferred_element_type=jnp.float32
    )
    return result.reshape(left.shape[:-1] + (weight.shape[0],))


def weight_term(left, right, grad_scale):
    left_rows = left.reshape(-1, left.shape[-1])
    right_rows = right.reshape(-1, right.shape[-1])

    def term_rows(start, count):
        column_part = lax.dynamic_slice_in_dim(left_rows, start, count, 1)
        product = lax.dot_general(
            column_part, right_rows, (((0,), (0,)), ((), ())), preferred_element_type=jnp.float32
        )
        return product * grad_scale

    return term_rows


def split_heads(packed, head_count):
    return packed.reshape(packed.shape[:-1] + (head_count, packed.shape[-1] // head_count))


def heads_major(tensor):
    videos, seq_len, head_count, head_width = tensor.shape
    return tensor.transpose(0, 2, 1, 3).reshape(videos * head_count, seq_len, head_width)


def heads_minor(tensor, videos):
    merged, seq_len, head_width = tensor.shape
    return tensor.reshape(videos, merged // videos, seq_len, head_width).transpose(0, 2, 1, 3)


def attend_head(triple):
    queries, key_rows, values = triple
    seq_len, head_width = queries.shape
    block_size = min(block_limit, seq_len)
    score_factor = temper / math.sqrt(head_width)
    values_wide = values.astype(jnp.float32)

    def one_block(query_rows):
        scores = jnp.dot(query_rows, key_rows.T, preferred_element_type=jnp.float32) * score_factor
        softmaxed = jax.nn.softmax(scores, axis=-1)
        return jnp.dot(softmaxed, values_wide, precision=lax.Precision.DEFAULT).astype(jnp.bfloat16)

    attended = lax.map(one_block, queries.reshape(seq_len // block_size, block_size, head_width))
    return attended.reshape(seq_len, head_width)


def attend_back(quadruple):
    queries, key_rows, values, upstream = quadruple
    seq_len, head_width = queries.shape
    block_size = min(block_limit, seq_len)
    score_factor = temper / math.sqrt(head_width)
    keys_wide = key_rows.astype(jnp.float32)

    def one_block(running, block_pair):
        query_rows, grad_rows = block_pair
        scores = jnp.dot(query_rows, key_rows.T, preferred_element_type=jnp.float32) * score_factor
        softmaxed = jax.nn.softmax(scores, axis=-1)
        dprobs = jnp.dot(grad_rows, values.T, preferred_element_type=jnp.float32)
        dscores = (
            softmaxed
            * (dprobs - jnp.sum(softmaxed * dprobs, axis=-1, keepdims=True))
            * score_factor
        )
        dquery = jnp.dot(dscores, keys_wide, precision=lax.Precision.DEFAULT)
        grad_keys = running[0] + jnp.dot(
            dscores.T, query_rows.astype(jnp.float32), precision=lax.Precision.DEFAULT
        )
        dvalues = running[1] + jnp.dot(
            softmaxed.T, grad_rows.astype(jnp.float32), precision=lax.Precision.DEFAULT
        )
        return ((grad_keys, dvalues), dquery)

    zero_rows = jnp.zeros((seq_len, head_width), jnp.float32)
    count = seq_len // block_size
    blocks = (
        queries.reshape(count, block_size, head_width),
        upstream.reshape(count, block_size, head_width),
    )
    (grad_keys, dvalues), dquery = lax.scan(one_block, (zero_rows, zero_rows), blocks)
    return (
        dquery.reshape(seq_len, head_width).astype(jnp.bfloat16),
        grad_keys.astype(jnp.bfloat16),
        dvalues.astype(jnp.bfloat16),
    )


def attend_all(queries, key_rows, values):
    attended = lax.map(
        attend_head, (heads_major(queries), heads_major(key_rows), heads_major(values))
    )
    return heads_minor(attended, queries.shape[0])


def attend_all_back(queries, key_rows, values, upstream):
    grad_heads = lax.map(
        attend_back,
        (heads_major(queries), heads_major(key_rows), heads_major(values), heads_major(upstream)),
    )
    return tuple((heads_minor(grad_piece, queries.shape[0]) for grad_piece in grad_heads))


def body(tokens, modulation, w_qkv, w_out, w_in, w_back, out_grad):
    videos, local_seq, model_width = tokens.shape
    layers = w_qkv.shape[0]
    own_width = w_qkv.shape[3]
    own_heads = own_width // HEAD_DIM
    grad_scale = 1.0 / math.sqrt(videos * local_seq * lax.axis_size("fsdp") * lax.axis_size(SP))
    stream = tokens.astype(jnp.float32)
    stored = []
    fetched = []
    for layer_index in range(layers):
        weights = one_gather(
            (w_qkv[layer_index], w_out[layer_index], w_in[layer_index], w_back[layer_index]),
            "fsdp",
            (0, 1, 0, 1),
        )
        fetched.append(weights)
        whole_qkv, whole_out, whole_in, whole_back = weights
        joint = whole_qkv.reshape(model_width, 3 * own_width)
        layer_mod = modulation[:, layer_index][:, :, None, :]
        normed_first, rstd_first = normalize(stream)
        input_first = (normed_first * (1.0 + layer_mod[:, 1]) + layer_mod[:, 0]).astype(
            jnp.bfloat16
        )
        first_rows = lax.all_gather(input_first, SP, axis=1, tiled=True)
        packed = project(first_rows, joint).astype(jnp.bfloat16)
        queries = split_heads(packed[..., :own_width], own_heads)
        key_rows = split_heads(packed[..., own_width : 2 * own_width], own_heads)
        values = split_heads(packed[..., 2 * own_width :], own_heads)
        attended = attend_all(queries, key_rows, values).reshape(videos, -1, own_width)
        attn_part = sum_by_axis(
            project(attended, whole_out).astype(jnp.bfloat16), SP, (1, 0), 1
        ).astype(jnp.float32)
        middle = stream + layer_mod[:, 2] * attn_part
        normed_second, rstd_second = normalize(middle)
        input_second = (normed_second * (1.0 + layer_mod[:, 4]) + layer_mod[:, 3]).astype(
            jnp.bfloat16
        )
        second_rows = lax.all_gather(input_second, SP, axis=1, tiled=True)
        hidden = project(second_rows, whole_in)
        activated = gelu_tanh(hidden).astype(jnp.bfloat16)
        ffn_part = sum_by_axis(
            project(activated, whole_back).astype(jnp.bfloat16), SP, (1, 0), 1
        ).astype(jnp.float32)
        stream = middle + layer_mod[:, 5] * ffn_part
        stored.append(
            (
                normed_first,
                rstd_first,
                first_rows,
                queries,
                key_rows,
                values,
                attended,
                normed_second,
                rstd_second,
                second_rows,
                hidden,
                activated,
            )
        )
    final_out = stream.astype(jnp.bfloat16)
    stream_grad = out_grad.astype(jnp.float32)
    results = [None] * layers
    for layer_index in range(layers - 1, -1, -1):
        (
            normed_first,
            rstd_first,
            first_rows,
            queries,
            key_rows,
            values,
            attended,
            normed_second,
            rstd_second,
            second_rows,
            hidden,
            activated,
        ) = stored[layer_index]
        whole_qkv, whole_out, whole_in, whole_back = fetched[layer_index]
        joint = whole_qkv.reshape(model_width, 3 * own_width)
        layer_mod = modulation[:, layer_index][:, :, None, :]
        down_grad = (layer_mod[:, 5] * stream_grad).astype(jnp.bfloat16)
        down_rows = lax.all_gather(down_grad, SP, axis=1, tiled=True)
        back_hidden = project_back(down_rows, whole_back)
        unused, pullback = jax.vjp(gelu_tanh, hidden)
        up_grad = pullback(back_hidden)[0].astype(jnp.bfloat16)
        back_second = sum_by_axis(
            project_back(up_grad, whole_in).astype(jnp.bfloat16), SP, (1, 0), 1
        ).astype(jnp.float32)
        stream_grad = stream_grad + norm_back(
            normed_second, rstd_second, back_second * (1.0 + layer_mod[:, 4])
        )
        attn_grad = (layer_mod[:, 2] * stream_grad).astype(jnp.bfloat16)
        attn_rows = lax.all_gather(attn_grad, SP, axis=1, tiled=True)
        mixed_grad = split_heads(project_back(attn_rows, whole_out).astype(jnp.bfloat16), own_heads)
        grad_query, grad_keys, grad_values = attend_all_back(queries, key_rows, values, mixed_grad)
        packed_grad = jnp.concatenate(
            [
                grad_query.reshape(videos, -1, own_width),
                grad_keys.reshape(videos, -1, own_width),
                grad_values.reshape(videos, -1, own_width),
            ],
            axis=-1,
        )
        back_first = lax.psum_scatter(
            project_back(packed_grad, joint).astype(jnp.bfloat16),
            SP,
            scatter_dimension=1,
            tiled=True,
        ).astype(jnp.float32)
        stream_grad = stream_grad + norm_back(
            normed_first, rstd_first, back_first * (1.0 + layer_mod[:, 1])
        )
        term_qkv = weight_term(first_rows, packed_grad, grad_scale)
        term_out = weight_term(attn_rows, attended, grad_scale)
        term_in = weight_term(second_rows, up_grad, grad_scale)
        term_back = weight_term(down_rows, activated, grad_scale)
        full_terms = (
            term_qkv(0, model_width),
            term_out(0, model_width),
            term_in(0, model_width),
            term_back(0, model_width),
        )
        sum_qkv, sum_out, sum_in, sum_back = tuple(
            (
                part.astype(jnp.float32)
                for part in sum_packed(
                    (
                        full_terms[0].astype(jnp.bfloat16),
                        full_terms[1].astype(jnp.bfloat16),
                        full_terms[2].astype(jnp.bfloat16),
                        full_terms[3].astype(jnp.bfloat16),
                    ),
                    "fsdp",
                    (0, 0, 0, 0),
                )
            )
        )
        results[layer_index] = (
            sum_qkv.reshape(sum_qkv.shape[0], 3, own_width),
            sum_out.T,
            sum_in,
            sum_back.T,
        )
    grad_qkv = jnp.stack([results[index][0] for index in range(layers)])
    grad_out = jnp.stack([results[index][1] for index in range(layers)])
    grad_in = jnp.stack([results[index][2] for index in range(layers)])
    grad_back = jnp.stack([results[index][3] for index in range(layers)])
    return (final_out, stream_grad, grad_qkv, grad_out, grad_in, grad_back)


def solution(mesh):
    torus = Mesh(mesh.devices.reshape(mesh.shape["fsdp"], 2, 2), ("fsdp", "sp_0", "sp_1"))
    return jax.shard_map(
        body,
        mesh=torus,
        in_specs=(
            P("fsdp", SP, None),
            P("fsdp", None, None, None),
            P(None, "fsdp", None, SP),
            P(None, SP, "fsdp"),
            P(None, "fsdp", SP),
            P(None, SP, "fsdp"),
            P("fsdp", SP, None),
        ),
        out_specs=(
            P("fsdp", SP, None),
            P("fsdp", SP, None),
            P(None, "fsdp", None, SP),
            P(None, SP, "fsdp"),
            P(None, "fsdp", SP),
            P(None, SP, "fsdp"),
        ),
        check_vma=False,
    )
```

profile of v0, /device:TPU:0, one launch (start us, length us, event | category | flops | bytes accessed | tf_op | source)
XLA Modules:
  0.0 1303.5 jit_solution(8247963021903286426)
XLA Ops:
  15.2 139.5 %all-gather.15.cloned.1.call-done = bf16[7077888]{0:T(1024)(128)(2,1)} async-done(((bf16[221184]{0:T(1024)(128)(2,1)}), bf16[7077888]{0:T(1024)(128)(2,1)}) %all-gather.15.cloned.1.call-update) | async-done | bytes 14155792 | tf_op jit(solution)/shard_map/all_gather | solution.py:26
  154.7 12.9 reshape.778
  172.7 6.6 all-gather.7.cloned.1.call-done
  179.3 4.7 fusion.57
  187.6 4.2 reshape.748
  191.8 3.2 copy.33
  197.8 13.1 %reduce-scatter.8.cloned.1.call-done = bf16[2,1,128,1536]{3,2,1,0:T(8,128)(2,1)} async-done(((bf16[4,1,128,1536]{3,2,1,0:T(8,128)(2,1)}), bf16[2,1,128,1536]{3,2,1,0:T(8,128)(2,1)}) %reduce-scatter.8.cloned.1.call-update) | async-done | bytes 786448 | tf_op jit(solution)/shard_map/reduce_scatter | solution.py:39
  211.0 23.5 %reduce-scatter.10.cloned.1.call-done = bf16[1,1,128,1536]{3,2,1,0:T(8,128)(2,1)} async-done(((bf16[2,1,128,1536]{3,2,1,0:T(8,128)(2,1)}), bf16[1,1,128,1536]{3,2,1,0:T(8,128)(2,1)}) %reduce-scatter.10.cloned.1.call-update) | async-done | bytes 393232 | tf_op jit(solution)/shard_map/reduce_scatter | solution.py:39
  240.1 8.1 fusion.111
  248.2 6.0 reshape_reshape.8
  254.2 15.1 %reshape.753 = bf16[32,1536,48]{2,1,0:T(8,128)(2,1)} reshape(bf16[32,73728]{1,0:T(8,128)(2,1)} %get-tuple-element.184) | data formatting | bytes 9437184 | tf_op jit(solution)/shard_map/reshape | solution.py:28
  269.3 12.0 copy.35
  281.3 7.2 fusion.68
  288.5 3.6 all-gather.11.cloned.1.call-done
  292.1 8.0 fusion.52
  304.7 6.1 fusion.55
  312.5 5.1 reduce-scatter.16.cloned.1.call-done
  317.6 15.5 %reduce-scatter.12.cloned.1.call-done = bf16[2,1,128,1536]{3,2,1,0:T(8,128)(2,1)} async-done(((bf16[4,1,128,1536]{3,2,1,0:T(8,128)(2,1)}), bf16[2,1,128,1536]{3,2,1,0:T(8,128)(2,1)}) %reduce-scatter.12.cloned.1.call-update) | async-done | bytes 786448 | tf_op jit(solution)/shard_map/reduce_scatter | solution.py:39
  333.2 6.7 fusion.43
  339.9 16.9 %reduce-scatter.18.cloned.1.call-done = bf16[1,1,128,1536]{3,2,1,0:T(8,128)(2,1)} async-done(((bf16[2,1,128,1536]{3,2,1,0:T(8,128)(2,1)}), bf16[1,1,128,1536]{3,2,1,0:T(8,128)(2,1)}) %reduce-scatter.18.cloned.1.call-update) | async-done | bytes 393232 | tf_op jit(solution)/shard_map/reduce_scatter | solution.py:39
  358.2 21.7 %reduce-scatter.14.cloned.1.call-done = bf16[1,1,128,1536]{3,2,1,0:T(8,128)(2,1)} async-done(((bf16[2,1,128,1536]{3,2,1,0:T(8,128)(2,1)}), bf16[1,1,128,1536]{3,2,1,0:T(8,128)(2,1)}) %reduce-scatter.14.cloned.1.call-update) | async-done | bytes 393232 | tf_op jit(solution)/shard_map/reduce_scatter | solution.py:39
  415.0 3.3 fusion.44
  449.1 28.3 %stack.567 = bf16[32,73728]{1,0:T(8,128)(2,1)} concatenate(bf16[1,73728]{1,0:T(2,128)(2,1)} %bitcast.775, bf16[1,73728]{1,0:T(2,128)(2,1)} %bitcast.776, bf16[1,73728]{1,0:T(2,128)(2,1)} %bitcast.777, bf16[1,73728]{1,0:T(2,128)(2,1)} %bitcast.778, bf16[1,73728]{1,0:T(2,128)(2,1)} %bitcast.779, bf16[1,73728]{1,0:T(2,128)(2,1)} %bitcast.780, bf16[1,73728]{1,0:T(2,128)(2,1)} %bitcast.781, ...), dimensions={0} | concatenate | bytes 9437184 | tf_op jit(solution)/shard_map/stack | solution.py:44
  477.4 28.6 %stack.600 = bf16[32,73728]{1,0:T(8,128)(2,1)} concatenate(bf16[1,73728]{1,0:T(2,128)(2,1)} %bitcast.807, bf16[1,73728]{1,0:T(2,128)(2,1)} %bitcast.808, bf16[1,73728]{1,0:T(2,128)(2,1)} %bitcast.809, bf16[1,73728]{1,0:T(2,128)(2,1)} %bitcast.810, bf16[1,73728]{1,0:T(2,128)(2,1)} %bitcast.811, bf16[1,73728]{1,0:T(2,128)(2,1)} %bitcast.812, bf16[1,73728]{1,0:T(2,128)(2,1)} %bitcast.813, ...), dimensions={0} | concatenate | bytes 9437184 | tf_op jit(solution)/shard_map/stack | solution.py:44
  511.9 24.3 %while.25 = (s32[]{:T(128)}, bf16[3,512,128]{1,2,0:T(8,128)(2,1)}, bf16[3,512,128]{1,2,0:T(8,128)(2,1)}, bf16[3,512,128]{1,2,0:T(8,128)(2,1)}, bf16[3,512,128]{2...) while((s32[]{:T(128)}, bf16[3,512,128]{1,2,0:T(8,128)(2,1)}, ...), condition=%wide.region_20.21_spmd, body=%wide.region_16.20_spmd.sunk | while | flops 340982272 | bytes 16547457 | solution.py:187
  536.3 4.0 fusion.45
  545.1 3.5 fusion.58
  600.0 23.8 %stack.501 = bf16[32,55296]{1,0:T(8,128)(2,1)} concatenate(bf16[1,55296]{1,0:T(2,128)(2,1)} %bitcast.848, bf16[1,55296]{1,0:T(2,128)(2,1)} %bitcast.849, bf16[1,55296]{1,0:T(2,128)(2,1)} %bitcast.850, bf16[1,55296]{1,0:T(2,128)(2,1)} %bitcast.851, bf16[1,55296]{1,0:T(2,128)(2,1)} %bitcast.839, bf16[1,55296]{1,0:T(2,128)(2,1)} %bitcast.840, bf16[1,55296]{1,0:T(2,128)(2,1)} %bitcast.841, ...), dimensions={0} | concatenate | bytes 7077888 | tf_op jit(solution)/shard_map/stack | solution.py:44
  623.8 9.1 stack.534
  632.9 31.7 %pad_maximum_fusion = bf16[32,221184]{1,0:T(8,128)(2,1)} fusion(bf16[32,73728]{1,0:T(8,128)(2,1)} %stack.600, bf16[32,73728]{1,0:T(8,128)(2,1)} %stack.567, bf16[32,18432]{1,0:T(8,128)(2,1)S(1)} %stack.534, bf16[32,55296]{1,0:T(8,128)(2,1)} %stack.501), kind=kLoop, calls=%fused_computation.54 | loop fusion | flops 56623104 | bytes 28311552 | tf_op jit(solution)/shard_map/concatenate | solution.py:55
  669.4 615.7 %all-reduce.3.cloned.1.call-done = bf16[32,221184]{1,0:T(8,128)(2,1)} async-done(((bf16[32,221184]{1,0:T(8,128)(2,1)}), bf16[32,221184]{1,0:T(8,128)(2,1)}) %all-reduce.3.cloned.1.call-update) | async-done | bytes 14155792
  1285.1 4.4 fusion.101
  (418 shorter events, 199.1 us)
Async XLA Ops:
  7.2 147.5 %all-gather.15.cloned.1.call-start = ((), (), s32[]{:S(2)}) async-start(), calls=%async_computation.18 | async-start | bytes 14598144 | tf_op jit(solution)/shard_map/all_gather | solution.py:26
  12.9 166.3 %all-gather.7.cloned.1.call-start = ((), (), s32[]{:S(2)}) async-start(), calls=%async_computation.7 | async-start | bytes 1966080 | tf_op jit(solution)/shard_map/all_gather | solution.py:217
  13.6 141.1 %copy-start.51 = (f32[1536]{0:T(1024)}, f32[1536]{0:T(1024)S(1)}, u32[]{:S(2)}) copy-start(f32[1536]{0:T(1024)S(1)} %get-tuple-element.145) | copy-start | bytes 18436
  13.8 141.0 %copy-start.56 = (f32[128]{0:T(128)}, f32[128]{0:T(128)S(1)}, u32[]{:S(2)}) copy-start(f32[128]{0:T(128)S(1)} %broadcast_multiply_fusion.5) | copy-start | bytes 1540
  14.1 140.7 %copy-start.58 = (f32[128]{0:T(128)}, f32[128]{0:T(128)S(1)}, u32[]{:S(2)}) copy-start(f32[128]{0:T(128)S(1)} %add_rsqrt_fusion.1) | copy-start | bytes 1540
  15.1 195.8 %reduce-scatter.8.cloned.1.call-start = ((), (), s32[]{:S(2)}) async-start(), calls=%async_computation.8 | async-start | bytes 2359296 | tf_op jit(solution)/shard_map/reduce_scatter | solution.py:39
  196.4 38.0 %copy-start.1 = (bf16[1,128,1536]{2,1,0:T(8,128)(2,1)S(1)}, bf16[1,128,1536]{2,1,0:T(8,128)(2,1)}, u32[]{:S(2)}) copy-start(bf16[1,128,1536]{2,1,0:T(8,128)(2,1)} %param.11) | copy-start | bytes 1179652
  196.4 40.5 %copy-start.55 = (f32[1536]{0:T(1024)S(1)}, f32[1536]{0:T(1024)}, u32[]{:S(2)}) copy-start(f32[1536]{0:T(1024)} %get-tuple-element.142) | copy-start | bytes 18436
  197.7 41.3 %copy-start.5 = (bf16[1,128,1536]{2,1,0:T(8,128)(2,1)S(1)}, bf16[1,128,1536]{2,1,0:T(8,128)(2,1)}, u32[]{:S(2)}) copy-start(bf16[1,128,1536]{2,1,0:T(8,128)(2,1)} %param.17) | copy-start | bytes 1179652
  197.7 41.3 %copy-start.53 = (f32[1536]{0:T(1024)S(1)}, f32[1536]{0:T(1024)}, u32[]{:S(2)}) copy-start(f32[1536]{0:T(1024)} %get-tuple-element.141) | copy-start | bytes 18436
  197.8 36.7 %reduce-scatter.10.cloned.1.call-start = ((), (), s32[]{:S(2)}) async-start(), calls=%async_computation.9 | async-start | bytes 1179648 | tf_op jit(solution)/shard_map/reduce_scatter | solution.py:39
  210.9 70.4 %all-gather.9.cloned.1.call-start = ((), (), s32[]{:S(2)}) async-start(), calls=%async_computation.10 | async-start | bytes 1966080 | tf_op jit(solution)/shard_map/all_gather | solution.py:231
  238.9 53.1 %all-gather.11.cloned.1.call-start = ((), (), s32[]{:S(2)}) async-start(), calls=%async_computation.13 | async-start | bytes 1966080 | tf_op jit(solution)/shard_map/all_gather | solution.py:276
  239.8 77.7 %reduce-scatter.16.cloned.1.call-start = ((), (), s32[]{:S(2)}) async-start(), calls=%async_computation.14 | async-start | bytes 2359296 | tf_op jit(solution)/shard_map/reduce_scatter | solution.py:39
  304.4 28.7 %reduce-scatter.12.cloned.1.call-start = ((), (), s32[]{:S(2)}) async-start(), calls=%async_computation.11 | async-start | bytes 2359296 | tf_op jit(solution)/shard_map/reduce_scatter | solution.py:39
  312.4 44.4 %reduce-scatter.18.cloned.1.call-start = ((), (), s32[]{:S(2)}) async-start(), calls=%async_computation.15 | async-start | bytes 1179648 | tf_op jit(solution)/shard_map/reduce_scatter | solution.py:39
  317.6 62.4 %reduce-scatter.14.cloned.1.call-start = ((), (), s32[]{:S(2)}) async-start(), calls=%async_computation.12 | async-start | bytes 1179648 | tf_op jit(solution)/shard_map/reduce_scatter | solution.py:39
  333.1 172.9 %all-gather.13.cloned.1.call-start = ((), (), s32[]{:S(2)}) async-start(), calls=%async_computation.16 | async-start | bytes 1966080 | tf_op jit(solution)/shard_map/all_gather | solution.py:287
  382.6 283.3 %reduce-scatter.20.cloned.1.call-start = ((), (), s32[]{:S(2)}) async-start(), calls=%async_computation.17 | async-start | bytes 1966080 | tf_op jit(solution)/shard_map/reduce_scatter | solution.py:298
  549.5 23.8 %copy-start.13 = (bf16[1,1,48,1152]{3,2,1,0:T(8,128)(2,1)S(1)}, bf16[1,1,48,1152]{3,2,1,0:T(8,128)(2,1)}, u32[]{:S(2)}) copy-start(bf16[1,1,48,1152]{3,2,1,0:T(8,128)(2,1)} %get-tuple-element.271) | copy-start | bytes 331780
  549.7 24.4 %copy-start.12 = (bf16[1,1,48,1152]{3,2,1,0:T(8,128)(2,1)S(1)}, bf16[1,1,48,1152]{3,2,1,0:T(8,128)(2,1)}, u32[]{:S(2)}) copy-start(bf16[1,1,48,1152]{3,2,1,0:T(8,128)(2,1)} %get-tuple-element.270) | copy-start | bytes 331780
  549.9 25.1 %copy-start.11 = (bf16[1,1,48,1152]{3,2,1,0:T(8,128)(2,1)S(1)}, bf16[1,1,48,1152]{3,2,1,0:T(8,128)(2,1)}, u32[]{:S(2)}) copy-start(bf16[1,1,48,1152]{3,2,1,0:T(8,128)(2,1)} %get-tuple-element.269) | copy-start | bytes 331780
  550.1 25.8 %copy-start.10 = (bf16[1,1,48,1152]{3,2,1,0:T(8,128)(2,1)S(1)}, bf16[1,1,48,1152]{3,2,1,0:T(8,128)(2,1)}, u32[]{:S(2)}) copy-start(bf16[1,1,48,1152]{3,2,1,0:T(8,128)(2,1)} %get-tuple-element.268) | copy-start | bytes 331780
  551.2 25.5 %copy-start.9 = (bf16[1,1,48,1152]{3,2,1,0:T(8,128)(2,1)S(1)}, bf16[1,1,48,1152]{3,2,1,0:T(8,128)(2,1)}, u32[]{:S(2)}) copy-start(bf16[1,1,48,1152]{3,2,1,0:T(8,128)(2,1)} %get-tuple-element.280) | copy-start | bytes 331780
  553.0 24.6 %copy-start.8 = (bf16[1,1,48,1152]{3,2,1,0:T(8,128)(2,1)S(1)}, bf16[1,1,48,1152]{3,2,1,0:T(8,128)(2,1)}, u32[]{:S(2)}) copy-start(bf16[1,1,48,1152]{3,2,1,0:T(8,128)(2,1)} %get-tuple-element.279) | copy-start | bytes 331780
  571.6 24.2 %copy-start.43 = (bf16[1,1,48,384]{3,2,1,0:T(8,128)(2,1)S(1)}, bf16[1,1,48,384]{3,2,1,0:T(8,128)(2,1)}, u32[]{:S(2)}) copy-start(bf16[1,1,48,384]{3,2,1,0:T(8,128)(2,1)} %get-tuple-element.317) | copy-start | bytes 110596
  571.6 24.9 %copy-start.42 = (bf16[1,1,48,384]{3,2,1,0:T(8,128)(2,1)S(1)}, bf16[1,1,48,384]{3,2,1,0:T(8,128)(2,1)}, u32[]{:S(2)}) copy-start(bf16[1,1,48,384]{3,2,1,0:T(8,128)(2,1)} %get-tuple-element.316) | copy-start | bytes 110596
  572.4 24.7 %copy-start.41 = (bf16[1,1,48,384]{3,2,1,0:T(8,128)(2,1)S(1)}, bf16[1,1,48,384]{3,2,1,0:T(8,128)(2,1)}, u32[]{:S(2)}) copy-start(bf16[1,1,48,384]{3,2,1,0:T(8,128)(2,1)} %get-tuple-element.315) | copy-start | bytes 110596
  572.4 25.4 %copy-start.40 = (bf16[1,1,48,384]{3,2,1,0:T(8,128)(2,1)S(1)}, bf16[1,1,48,384]{3,2,1,0:T(8,128)(2,1)}, u32[]{:S(2)}) copy-start(bf16[1,1,48,384]{3,2,1,0:T(8,128)(2,1)} %get-tuple-element.314) | copy-start | bytes 110596
  572.4 26.1 %copy-start.39 = (bf16[1,1,48,384]{3,2,1,0:T(8,128)(2,1)S(1)}, bf16[1,1,48,384]{3,2,1,0:T(8,128)(2,1)}, u32[]{:S(2)}) copy-start(bf16[1,1,48,384]{3,2,1,0:T(8,128)(2,1)} %get-tuple-element.313) | copy-start | bytes 110596
  573.3 25.9 %copy-start.38 = (bf16[1,1,48,384]{3,2,1,0:T(8,128)(2,1)S(1)}, bf16[1,1,48,384]{3,2,1,0:T(8,128)(2,1)}, u32[]{:S(2)}) copy-start(bf16[1,1,48,384]{3,2,1,0:T(8,128)(2,1)} %get-tuple-element.312) | copy-start | bytes 110596
  600.0 685.1 %all-reduce.3.cloned.1.call-start = ((), (), s32[]{:S(2)}) async-start(), calls=%async_computation.19 | async-start | bytes 28311552
  (53 other events, 703.7 us)
Sparse Core Ops, SparseCore 0:
  13.1 141.6 all-gather.14
  157.0 22.2 all-gather.6
  197.9 12.9 reduce-scatter.7
  213.1 21.2 reduce-scatter.9
  239.1 25.3 all-gather.8
  266.5 25.5 all-gather.10
  304.5 12.9 reduce-scatter.15
  319.9 13.1 reduce-scatter.11
  335.5 21.2 reduce-scatter.17
  359.0 20.8 reduce-scatter.13
  382.7 25.3 all-gather.12
  600.1 24.5 reduce-scatter.19
  664.8 620.2 all-reduce.2
where the time goes:
time: 1320 us; the launch traced here: 1300 us
  waiting for transfers between devices  861 us (65%)
  local copies, waits for them, and re-layouts  298 us (23%)
  matrix products  67.9 us (5%)
  other arithmetic  58.8 us (4%)
  between operations  15 us (1%)
    unnamed x14, waiting for transfers between devices  616 us
    all_gather x1, waiting for transfers between devices, one_gather(): lines, at, gathered = (lax.all_gather(ravelled, axis), 0, [])  140 us
    unnamed x275, local copies, waits for them, and re-layouts  122 us
    reduce_scatter x6, waiting for transfers between devices, own_block(): blocks = lax.psum_scatter(blocks, axes[k], scatter_dimension=0, tiled=True)  95.7 us
    another operation x7, local copies, waits for them, and re-layouts, cut_along(): return jnp.stack(jnp.split(value, count, axis=dim))  90.1 us
    concatenate x1, other arithmetic, sum_packed(): lines = jnp.concatenate([b.reshape(count, -1) for b in blocks], axis=1)  31.7 us
  transfers between devices with their start and end apart: 13, of which 10 were waited for; matrix products, arithmetic and copies ran while one was open for 21% of the time, Pallas kernels for 0%

commit v1 on v0

v1 whole, which is shorter than its diff:
```python
import math

import jax
import jax.numpy as jnp
from jax import lax
from jax.experimental import pallas as pl
from jax.experimental.pallas import tpu as pltpu
from jax.sharding import Mesh
from jax.sharding import PartitionSpec as P

HEAD_DIM = 128
FSDP = ("fsdp_zy", "fsdp_x")
SP = ("sp_x", "sp_core")
SWAP = ((0, 1), (1, 0))

ln_eps = 1e-06
temper = 2.5
BF = jnp.bfloat16
F32 = jnp.float32


def normalize(stream):
    mean_part = jnp.mean(stream, axis=-1, keepdims=True)
    centred = stream - mean_part
    rstd = lax.rsqrt(jnp.mean(centred * centred, axis=-1, keepdims=True) + ln_eps)
    return (centred * rstd, rstd)


def norm_back(normed, rstd, incoming):
    first = jnp.mean(incoming, axis=-1, keepdims=True)
    second = jnp.mean(incoming * normed, axis=-1, keepdims=True)
    return rstd * (incoming - first - normed * second)


def gelu_tanh(hidden):
    return jax.nn.gelu(hidden, approximate=True)


def dot_nn(left, right):
    return jnp.dot(left, right, preferred_element_type=F32)


def dot_nt(left, right):
    return lax.dot_general(left, right, (((1,), (1,)), ((), ())), preferred_element_type=F32)


def dot_tn(left, right):
    return lax.dot_general(left, right, (((0,), (0,)), ((), ())), preferred_element_type=F32)


def swap(value, axis):
    return lax.ppermute(value, axis, SWAP)


def near_rows(own):
    return jnp.concatenate([own, swap(own, "sp_core")], axis=0)


def far_rows(own):
    across = swap(own, "sp_x")
    return jnp.concatenate([across, swap(across, "sp_core")], axis=0)


def core_sum(part):
    rows = part.shape[0] // 2
    given = swap(part[rows:].astype(BF), "sp_core")
    return part[:rows] + given.astype(F32)


def far_sum(part):
    return swap(core_sum(part).astype(BF), "sp_x").astype(F32)


def ordered(own, other, axis):
    first = jnp.concatenate([own, other], axis=0)
    second = jnp.concatenate([other, own], axis=0)
    return jnp.where(lax.axis_index(axis) == 0, first, second)


def attend_kernel(q_ref, k_ref, v_ref, o_ref):
    factor = temper / math.sqrt(HEAD_DIM)
    scores = dot_nt(q_ref[...], k_ref[...]) * factor
    lifted = jnp.exp(scores - jnp.max(scores, axis=-1, keepdims=True))
    probs = lifted / jnp.sum(lifted, axis=-1, keepdims=True)
    o_ref[...] = dot_nn(probs.astype(BF), v_ref[...]).astype(BF)


def attend(packed):
    rows, width = packed.shape
    heads = width // (3 * HEAD_DIM)
    block = (rows, HEAD_DIM)
    return pl.pallas_call(
        attend_kernel,
        grid=(heads,),
        in_specs=[
            pl.BlockSpec(block, lambda h: (0, h)),
            pl.BlockSpec(block, lambda h: (0, heads + h)),
            pl.BlockSpec(block, lambda h: (0, 2 * heads + h)),
        ],
        out_specs=pl.BlockSpec(block, lambda h: (0, h)),
        out_shape=jax.ShapeDtypeStruct((rows, heads * HEAD_DIM), BF),
        name="attend",
    )(packed, packed, packed)


def attend_back_kernel(q_ref, k_ref, v_ref, d_ref, o_ref):
    heads = pl.num_programs(0)
    head = pl.program_id(0)
    factor = temper / math.sqrt(HEAD_DIM)
    queries, keys, values, upstream = q_ref[...], k_ref[...], v_ref[...], d_ref[...]
    scores = dot_nt(queries, keys) * factor
    lifted = jnp.exp(scores - jnp.max(scores, axis=-1, keepdims=True))
    probs = lifted / jnp.sum(lifted, axis=-1, keepdims=True)
    dprobs = dot_nt(upstream, values)
    inner = jnp.sum(probs * dprobs, axis=-1, keepdims=True)
    dscores = (probs * (dprobs - inner) * factor).astype(BF)
    probs = probs.astype(BF)

    def put(place, value):
        at = pl.multiple_of((place * heads + head) * HEAD_DIM, HEAD_DIM)
        o_ref[:, pl.ds(at, HEAD_DIM)] = value.astype(BF)

    put(0, dot_nn(dscores, keys))
    put(1, dot_tn(dscores, queries))
    put(2, dot_tn(probs, upstream))


def attend_back(packed, upstream):
    rows, width = packed.shape
    heads = width // (3 * HEAD_DIM)
    block = (rows, HEAD_DIM)
    return pl.pallas_call(
        attend_back_kernel,
        grid=(heads,),
        in_specs=[
            pl.BlockSpec(block, lambda h: (0, h)),
            pl.BlockSpec(block, lambda h: (0, heads + h)),
            pl.BlockSpec(block, lambda h: (0, 2 * heads + h)),
            pl.BlockSpec(block, lambda h: (0, h)),
        ],
        out_specs=pl.BlockSpec((rows, width), lambda h: (0, 0)),
        out_shape=jax.ShapeDtypeStruct((rows, width), BF),
        name="attend_back",
    )(packed, packed, packed, upstream)


def scatter_sum(term):
    rows = lax.psum_scatter(term, "fsdp_zy", scatter_dimension=0, tiled=True)
    half = rows.shape[0] // 2
    low, high = rows[:half], rows[half:]
    at_low = lax.axis_index("fsdp_x") == 0
    given = swap(jnp.where(at_low, high, low), "fsdp_x")
    return jnp.where(at_low, low, high).astype(F32) + given.astype(F32)


def block_pass(tokens, layer_mod, w_qkv, w_out, w_in, w_back, out_grad, grad_scale):
    qkv_width, out_width, in_width = w_qkv.shape[1], w_out.shape[0], w_in.shape[1]
    own_weights = jnp.concatenate([w_qkv, w_out.T, w_in, w_back.T], axis=1)
    pair = ordered(own_weights, swap(own_weights, "fsdp_x"), "fsdp_x")
    cut = qkv_width + out_width
    attn_weights = lax.all_gather(pair[:, :cut], "fsdp_zy", axis=0, tiled=True)
    ffn_weights = lax.all_gather(pair[:, cut:], "fsdp_zy", axis=0, tiled=True)
    joint, out_rows = attn_weights[:, :qkv_width], attn_weights[:, qkv_width:]
    in_rows, back_rows = ffn_weights[:, :in_width], ffn_weights[:, in_width:]

    stream = tokens.astype(F32)
    normed_first, rstd_first = normalize(stream)
    input_first = (normed_first * (1.0 + layer_mod[1]) + layer_mod[0]).astype(BF)
    first_rows = jnp.concatenate([near_rows(input_first), far_rows(input_first)], axis=0)
    packed = dot_nn(first_rows, joint).astype(BF)
    attended = attend(packed)
    half = attended.shape[0] // 2
    attn_part = far_sum(dot_nt(attended[half:], out_rows))
    attn_part = attn_part + core_sum(dot_nt(attended[:half], out_rows))
    middle = stream + layer_mod[2] * attn_part
    normed_second, rstd_second = normalize(middle)
    input_second = (normed_second * (1.0 + layer_mod[4]) + layer_mod[3]).astype(BF)
    second_rows = jnp.concatenate([near_rows(input_second), far_rows(input_second)], axis=0)
    hidden = dot_nn(second_rows, in_rows)
    activated, pullback = jax.vjp(gelu_tanh, hidden)
    activated = activated.astype(BF)
    ffn_part = far_sum(dot_nt(activated[half:], back_rows))
    ffn_part = ffn_part + core_sum(dot_nt(activated[:half], back_rows))
    final_out = (middle + layer_mod[5] * ffn_part).astype(BF)

    stream_grad = out_grad.astype(F32)
    down_grad = (layer_mod[5] * stream_grad).astype(BF)
    down_rows = jnp.concatenate([near_rows(down_grad), far_rows(down_grad)], axis=0)
    up_grad = pullback(dot_nn(down_rows, back_rows))[0].astype(BF)
    back_second = far_sum(dot_nt(up_grad[half:], in_rows))
    back_second = back_second + core_sum(dot_nt(up_grad[:half], in_rows))
    term_back = (dot_tn(down_rows, activated) * grad_scale).astype(BF)
    term_in = (dot_tn(second_rows, up_grad) * grad_scale).astype(BF)
    sum_ffn = scatter_sum(jnp.concatenate([term_in, term_back], axis=1))
    stream_grad = stream_grad + norm_back(
        normed_second, rstd_second, back_second * (1.0 + layer_mod[4])
    )
    attn_grad = (layer_mod[2] * stream_grad).astype(BF)
    attn_rows = jnp.concatenate([near_rows(attn_grad), far_rows(attn_grad)], axis=0)
    mixed_grad = dot_nn(attn_rows, out_rows).astype(BF)
    packed_grad = attend_back(packed, mixed_grad)
    term_out = (dot_tn(attn_rows, attended) * grad_scale).astype(BF)
    term_qkv = (dot_tn(first_rows, packed_grad) * grad_scale).astype(BF)
    sum_attn = scatter_sum(jnp.concatenate([term_qkv, term_out], axis=1))
    back_first = far_sum(dot_nt(packed_grad[half:], joint))
    back_first = back_first + core_sum(dot_nt(packed_grad[:half], joint))
    stream_grad = stream_grad + norm_back(
        normed_first, rstd_first, back_first * (1.0 + layer_mod[1])
    )
    return (
        final_out,
        stream_grad,
        sum_attn[:, :qkv_width],
        sum_attn[:, qkv_width:].T,
        sum_ffn[:, :in_width],
        sum_ffn[:, in_width:].T,
    )


def body(tokens, modulation, w_qkv, w_out, w_in, w_back, out_grad):
    local_seq = tokens.shape[1]
    own_width = w_qkv.shape[3]
    grad_scale = 1.0 / math.sqrt(local_seq * lax.axis_size(FSDP) * lax.axis_size(SP))
    final_out, input_grad, grad_qkv, grad_out, grad_in, grad_back = block_pass(
        tokens[0],
        modulation[0, 0],
        w_qkv[0].reshape(-1, 3 * own_width),
        w_out[0],
        w_in[0],
        w_back[0],
        out_grad[0],
        grad_scale,
    )
    return (
        final_out[None],
        input_grad[None],
        grad_qkv.reshape(1, -1, 3, own_width),
        grad_out[None],
        grad_in[None],
        grad_back[None],
    )


def solution(mesh):
    torus = Mesh(
        mesh.devices.reshape(mesh.shape["fsdp"] // 2, 2, 2, 2),
        ("fsdp_zy", "fsdp_x", "sp_x", "sp_core"),
    )
    return jax.shard_map(
        body,
        mesh=torus,
        in_specs=(
            P(FSDP, SP, None),
            P(FSDP, None, None, None),
            P(None, FSDP, None, SP),
            P(None, SP, FSDP),
            P(None, FSDP, SP),
            P(None, SP, FSDP),
            P(FSDP, SP, None),
        ),
        out_specs=(
            P(FSDP, SP, None),
            P(FSDP, SP, None),
            P(None, FSDP, None, SP),
            P(None, SP, FSDP),
            P(None, FSDP, SP),
            P(None, SP, FSDP),
        ),
        check_vma=False,
    )
```

time: 1320 us -> 434 us (0.33)
  waiting for transfers between devices: 861 us -> 271 us
  local copies, waits for them, and re-layouts: 298 us -> 32.1 us
  other arithmetic: 58.8 us -> 23.5 us
  starting transfers between devices: 1.46 us -> 24.9 us
  matrix products: 67.9 us -> 48.5 us
    unnamed x14 -> x6, waiting for transfers between devices: 616 us -> 110 us
    another operation x21 -> x0, local copies, waits for them, and re-layouts: 105 us -> none  [the longest x7 90.1 us: cut_along(): return jnp.stack(jnp.split(value, count, axis=dim))]
    unnamed x275 -> x88, local copies, waits for them, and re-layouts: 122 us -> 26.6 us
    reduce_scatter x7 -> x0, waiting for transfers between devices: 95.7 us -> none  [the longest x6 95.7 us: own_block(): blocks = lax.psum_scatter(blocks, axes[k], scatter_dimension=0, tiled=True)]
    ppermute x0 -> x27, waiting for transfers between devices: none -> 86.7 us  [swap(): return lax.ppermute(value, axis, SWAP)]
    all_gather x5 -> x2, waiting for transfers between devices: 150 us -> 74.5 us  [the longest x1 43 us: block_pass(): attn_weights = lax.all_gather(pair[:, :cut], 'fsdp_zy', axis=0, tiled=True)]
    ppermute x0 -> x27, starting transfers between devices: none -> 24.5 us  [swap(): return lax.ppermute(value, axis, SWAP)]
    reshape x2 -> x0, local copies, waits for them, and re-layouts: 19.4 us -> none  [one_gather(): blocks = lines[:, at:at + a.size].reshape(-1, *a.shape)]
  transfers between devices with their start and end apart: 13 -> 31, of which waited for: 10 -> 16; matrix products, arithmetic and copies ran while one was open for 21% -> 17% of each run, Pallas kernels for 0% -> 1%
where the time goes in v1:
time: 434 us; the launch traced here: 426 us
  waiting for transfers between devices  271 us (62%)
  matrix products  48.5 us (11%)
  local copies, waits for them, and re-layouts  32.1 us (7%)
  starting transfers between devices  24.9 us (6%)
  other arithmetic  23.5 us (5%)
  between operations  15 us (3%)
  Pallas kernels  11.2 us (3%)
    unnamed x6, waiting for transfers between devices  110 us
    ppermute x27, waiting for transfers between devices, swap(): return lax.ppermute(value, axis, SWAP)  86.7 us
    all_gather x1, waiting for transfers between devices, block_pass(): attn_weights = lax.all_gather(pair[:, :cut], 'fsdp_zy', axis=0, tiled=True)  43 us
    all_gather x1, waiting for transfers between devices, block_pass(): ffn_weights = lax.all_gather(pair[:, cut:], 'fsdp_zy', axis=0, tiled=True)  31.5 us
    unnamed x88, local copies, waits for them, and re-layouts  26.6 us
    ppermute x27, starting transfers between devices, swap(): return lax.ppermute(value, axis, SWAP)  24.5 us
    dot_general x4, matrix products, dot_nn(): return jnp.dot(left, right, preferred_element_type=F32)  20.1 us
    dot_general x8, matrix products, dot_nt(): lax.dot_general(left, right, (((1,), (1,)), ((), ())), preferred_element_...  16 us
  transfers between devices with their start and end apart: 31, of which 16 were waited for; matrix products, arithmetic and copies ran while one was open for 17% of the time, Pallas kernels for 1%

profile of v1, /device:TPU:0, one launch (start us, length us, event | category | flops | bytes accessed | tf_op | source)
XLA Modules:
  0.0 426.3 jit_solution(9301414642431365087)
XLA Ops:
  9.3 3.2 collective-permute-start.3
  12.5 10.4 %collective-permute-done.3 = bf16[48,4608]{1,0:T(8,128)(2,1)S(1)} collective-permute-done((bf16[48,4608]{1,0:T(8,128)(2,1)S(1)}, bf16[48,4608]{1,0:T(8,128)(2,1)S(1)}, u32[]{:S(2)}, u32[]{:S(2)}) %collective-permute-start.3) | collective-permute-done | bytes 442400 | tf_op jit(solution)/shard_map/ppermute | solution.py:52
  28.7 8.0 %collective-permute-done.1 = bf16[128,1536]{1,0:T(8,128)(2,1)S(1)} collective-permute-done((bf16[128,1536]{1,0:T(8,128)(2,1)S(1)}, bf16[128,1536]{1,0:T(8,128)(2,1)S(1)}, u32[]{:S(2)}, u32[]{:S(2)}) %collective-permute-start.1) | collective-permute-done | bytes 393248 | tf_op jit(solution)/shard_map/ppermute | solution.py:52
  38.4 43.0 %all-gather.3.cloned.1.call-done = bf16[1536,1536]{1,0:T(8,128)(2,1)} async-done(((bf16[96,1536]{1,0:T(8,128)(2,1)}), bf16[1536,1536]{1,0:T(8,128)(2,1)}) %all-gather.3.cloned.1.call-update) | async-done | bytes 4718608 | tf_op jit(solution)/shard_map/all_gather | solution.py:161
  81.4 5.2 %convolution_convert_fusion.q_ref.k_ref.v_ref = bf16[512,1152]{1,0:T(8,128)(2,1)} fusion(bf16[1536,1536]{1,0:T(8,128)(2,1)} %all-gather.3.cloned.1.call-done, bf16[128,1536]{1,0:T(8,128)(2,1)S(1)} %collective-permute-done.2, bf16[128,1536]{1,0:T(8,128)(2,1)S(1)} %collective-permute-done.1, bf16[128,1536]{1,0:T(8,128)(2,1)S(1)} %collective-permute-done, ...), kind=kOutput, calls=%fused_computation.31 | convolution fusion | flops 1818820608 | bytes 6291456 | tf_op jit(solution)/shard_map/dot_general | solution.py:40
  86.7 4.7 %attend.1 = bf16[512,384]{1,0:T(8,128)(2,1)} custom-call(bf16[512,1152]{1,0:T(8,128)(2,1)} %convolution_convert_fusion.q_ref.k_ref.v_ref, bf16[512,1152]{1,0:T(8,128)(2,1)} %convolution_convert_fusion.q_ref.k_ref.v_ref, bf16[512,1152]{1,0:T(8,128)(2,1)} %convolution_convert_fusion.q_ref.k_ref.v_ref), custom_call_target="tpu_custom_call" | custom-call | tf_op jit(solution)/shard_map/attend/pallas_call | solution.py:92
  97.7 9.6 %collective-permute-done.5 = bf16[128,1536]{1,0:T(8,128)(2,1)S(1)} collective-permute-done((bf16[128,1536]{1,0:T(8,128)(2,1)S(1)}, bf16[128,1536]{1,0:T(8,128)(2,1)S(1)}, u32[]{:S(2)}, u32[]{:S(2)}) %collective-permute-start.5) | collective-permute-done | bytes 393248 | tf_op jit(solution)/shard_map/ppermute | solution.py:52
  110.4 9.8 %collective-permute-done.8 = bf16[128,1536]{1,0:T(8,128)(2,1)S(1)} collective-permute-done((bf16[128,1536]{1,0:T(8,128)(2,1)S(1)}, bf16[128,1536]{1,0:T(8,128)(2,1)S(1)}, u32[]{:S(2)}, u32[]{:S(2)}) %collective-permute-start.8) | collective-permute-done | bytes 393248 | tf_op jit(solution)/shard_map/ppermute | solution.py:52
  120.7 6.3 %collective-permute-done.14 = bf16[128,1536]{1,0:T(8,128)(2,1)} collective-permute-done((bf16[128,1536]{1,0:T(8,128)(2,1)S(1)}, bf16[128,1536]{1,0:T(8,128)(2,1)}, u32[]{:S(2)}, u32[]{:S(2)}) %collective-permute-start.14) | collective-permute-done | bytes 393248 | tf_op jit(solution)/shard_map/ppermute | solution.py:52
  128.0 31.5 %all-gather.5.cloned.1.call-done = bf16[1536,3072]{1,0:T(8,128)(2,1)} async-done(((bf16[96,3072]{1,0:T(8,128)(2,1)}), bf16[1536,3072]{1,0:T(8,128)(2,1)}) %all-gather.5.cloned.1.call-update) | async-done | bytes 9437200 | tf_op jit(solution)/shard_map/all_gather | solution.py:162
  159.5 5.8 %multiply_convert_fusion = (bf16[512,1536]{1,0:T(8,128)(2,1)S(1)}, f32[512,1536]{1,0:T(8,128)S(1)}) fusion(bf16[1536,3072]{1,0:T(8,128)(2,1)} %all-gather.5.cloned.1.call-done, bf16[128,1536]{1,0:T(8,128)(2,1)} %collective-permute-done.9, bf16[128,1536]{1,0:T(8,128)(2,1)S(1)} %collective-permute-done.8, bf16[128,1536]{1,0:T(8,128)(2,1)} %copy-done.30, ...), kind=kOutput, calls=%fused_computation.29 | convolution fusion | flops 2429288448 | bytes 11010048 | tf_op jit(solution)/shard_map/dot_general | solution.py:40
  165.3 5.9 %fusion.21 = bf16[512,1536]{1,0:T(8,128)(2,1)S(1)} fusion(f32[512,1536]{1,0:T(8,128)S(1)} %get-tuple-element.48, bf16[1536,3072]{1,0:T(8,128)(2,1)S(1)} %copy-done.21, bf16[128,1536]{1,0:T(8,128)(2,1)} %collective-permute-done.15, bf16[128,1536]{1,0:T(8,128)(2,1)} %collective-permute-done.14, bf16[128,1536]{1,0:T(8,128)(2,1)} %collective-permute-done.13, ...), kind=kOutput, calls=%fused_computation.28 | convolution fusion | flops 2437939200 | bytes 11010048 | tf_op jit(solution)/shard_map/dot_general | solution.py:40
  181.9 8.9 %collective-permute-done.17 = bf16[128,1536]{1,0:T(8,128)(2,1)S(1)} collective-permute-done((bf16[128,1536]{1,0:T(8,128)(2,1)S(1)}, bf16[128,1536]{1,0:T(8,128)(2,1)S(1)}, u32[]{:S(2)}, u32[]{:S(2)}) %collective-permute-start.17) | collective-permute-done | bytes 393248 | tf_op jit(solution)/shard_map/ppermute | solution.py:52
  191.2 7.2 %collective-permute-done.11 = bf16[128,1536]{1,0:T(8,128)(2,1)S(1)} collective-permute-done((bf16[128,1536]{1,0:T(8,128)(2,1)S(1)}, bf16[128,1536]{1,0:T(8,128)(2,1)S(1)}, u32[]{:S(2)}, u32[]{:S(2)}) %collective-permute-start.11) | collective-permute-done | bytes 393248 | tf_op jit(solution)/shard_map/ppermute | solution.py:52
  201.2 8.8 %collective-permute-done.20 = bf16[128,1536]{1,0:T(8,128)(2,1)S(1)} collective-permute-done((bf16[128,1536]{1,0:T(8,128)(2,1)S(1)}, bf16[128,1536]{1,0:T(8,128)(2,1)S(1)}, u32[]{:S(2)}, u32[]{:S(2)}) %collective-permute-start.20) | collective-permute-done | bytes 393248 | tf_op jit(solution)/shard_map/ppermute | solution.py:52
  211.7 3.1 convolution_convert_fusion.1.d_ref
  214.9 6.5 %attend_back.1 = bf16[512,1152]{1,0:T(8,128)(2,1)} custom-call(bf16[512,1152]{1,0:T(8,128)(2,1)} %convolution_convert_fusion.q_ref.k_ref.v_ref, bf16[512,1152]{1,0:T(8,128)(2,1)} %convolution_convert_fusion.q_ref.k_ref.v_ref, bf16[512,1152]{1,0:T(8,128)(2,1)} %convolution_convert_fusion.q_ref.k_ref.v_ref, bf16[512,384]{1,0:T(8,128)(2,1)} %convolution_convert_fusion.1.d_ref), custom_call_target="tpu_custom_call" | custom-call | tf_op jit(solution)/shard_map/attend_back/pallas_call | solution.py:132
  221.4 2.2 fusion.24
  225.6 2.5 pad_maximum_fusion.1
  228.1 6.6 %copy.30 = bf16[1536,1536]{1,0:T(8,128)(2,1)} copy(bf16[1536,1536]{0,1:T(8,128)(2,1)} %pad_maximum_fusion.1) | data formatting | bytes 9437184
  235.7 4.6 %fusion.1 = bf16[1536,1536]{0,1:T(8,128)(2,1)S(1)} fusion(bf16[512,1536]{1,0:T(8,128)(2,1)} %copy-done.35, bf16[128,1536]{1,0:T(8,128)(2,1)} %collective-permute-done.15, bf16[128,1536]{1,0:T(8,128)(2,1)} %collective-permute-done.14, bf16[128,1536]{1,0:T(8,128)(2,1)} %collective-permute-done.13, bf16[128,1536]{1,0:T(8,128)(2,1)S(1)} %copy-done.5), kind=kOutput, calls=%fused_computation.5 | convolution fusion | flops 2426929152 | bytes 7864320 | tf_op jit(solution)/shard_map/dot_general | solution.py:48
  240.3 3.7 fusion
  244.0 12.3 %pad_maximum_fusion = bf16[1536,3072]{0,1:T(8,128)(2,1)} fusion(bf16[1536,1536]{0,1:T(8,128)(2,1)S(1)} %fusion.1, bf16[1536,1536]{0,1:T(8,128)(2,1)S(1)} %fusion), kind=kLoop, calls=%fused_computation.3 | loop fusion | flops 18874368 | bytes 18874368 | tf_op jit(solution)/shard_map/concatenate | solution.py:194
  256.3 12.6 %copy.32 = bf16[1536,3072]{1,0:T(8,128)(2,1)} copy(bf16[1536,3072]{0,1:T(8,128)(2,1)} %pad_maximum_fusion) | data formatting | bytes 18874368
  268.9 3.2 fusion.27
  272.4 3.2 fusion.25
  277.7 9.7 %collective-permute-done.23 = bf16[128,1536]{1,0:T(8,128)(2,1)S(1)} collective-permute-done((bf16[128,1536]{1,0:T(8,128)(2,1)S(1)}, bf16[128,1536]{1,0:T(8,128)(2,1)S(1)}, u32[]{:S(2)}, u32[]{:S(2)}) %collective-permute-start.23) | collective-permute-done | bytes 393248 | tf_op jit(solution)/shard_map/ppermute | solution.py:52
  289.0 24.6 %reduce-scatter.7.cloned.1.call-done = bf16[96,1536]{1,0:T(8,128)(2,1)} async-done(((bf16[1536,1536]{1,0:T(8,128)(2,1)}), bf16[96,1536]{1,0:T(8,128)(2,1)}) %reduce-scatter.7.cloned.1.call-update) | async-done | bytes 294928
  315.9 3.3 collective-permute-start.25
  319.2 85.1 %reduce-scatter.9.cloned.1.call-done = bf16[96,3072]{1,0:T(8,128)(2,1)} async-done(((bf16[1536,3072]{1,0:T(8,128)(2,1)}), bf16[96,3072]{1,0:T(8,128)(2,1)}) %reduce-scatter.9.cloned.1.call-update) | async-done | bytes 589840
  407.2 3.0 collective-permute-start.26
  412.1 4.5 %collective-permute-done.26 = bf16[48,3072]{1,0:T(8,128)(2,1)S(1)} collective-permute-done((bf16[48,3072]{1,0:T(8,128)(2,1)}, bf16[48,3072]{1,0:T(8,128)(2,1)S(1)}, u32[]{:S(2)}, u32[]{:S(2)}) %collective-permute-start.26) | collective-permute-done | bytes 294944 | tf_op jit(solution)/shard_map/ppermute | solution.py:52
  (188 shorter events, 52.2 us)
Async XLA Ops:
  7.2 74.3 %all-gather.3.cloned.1.call-start = ((), (), s32[]{:S(2)}) async-start(), calls=%async_computation.2 | async-start | bytes 5013504 | tf_op jit(solution)/shard_map/all_gather | solution.py:161
  9.3 13.7 %collective-permute-start.3 = (bf16[48,4608]{1,0:T(8,128)(2,1)S(1)}, bf16[48,4608]{1,0:T(8,128)(2,1)S(1)}, u32[]{:S(2)}, u32[]{:S(2)}) collective-permute-start(bf16[48,4608]{1,0:T(8,128)(2,1)S(1)} %pad_maximum_fusion.6), channel_id=1, source_target_pairs={{0,4},{4,0},{1,5},{5,1},{2,6},{6,2},{3,7},{7,3},{8,12},{12,8},{9,1... | collective-permute-start | bytes 1327112 | tf_op jit(solution)/shard_map/ppermute | solution.py:52
  25.0 134.4 %all-gather.5.cloned.1.call-start = ((), (), s32[]{:S(2)}) async-start(), calls=%async_computation.3 | async-start | bytes 10027008 | tf_op jit(solution)/shard_map/all_gather | solution.py:162
  25.9 287.7 %reduce-scatter.7.cloned.1.call-start = ((), (), s32[]{:S(2)}) async-start(), calls=%async_computation.4 | async-start | bytes 5013504
  26.1 81.8 %copy-start.10 = (f32[1536]{0:T(1024)}, f32[1536]{0:T(1024)S(1)}, u32[]{:S(2)}) copy-start(f32[1536]{0:T(1024)S(1)} %get-tuple-element.33) | copy-start | bytes 18436
  26.9 9.8 %collective-permute-start.1 = (bf16[128,1536]{1,0:T(8,128)(2,1)S(1)}, bf16[128,1536]{1,0:T(8,128)(2,1)S(1)}, u32[]{:S(2)}, u32[]{:S(2)}) collective-permute-start(bf16[128,1536]{1,0:T(8,128)(2,1)S(1)} %fusion.43), channel_id=1, source_target_pairs={{0,2},{2,0},{1,3},{3,1},{4,6},{6,4},{5,7},{7,5},{8,10},{10,8},{9,1... | collective-permute-start | bytes 1179656 | tf_op jit(solution)/shard_map/ppermute | solution.py:52
  28.7 8.0 %collective-permute-start = (bf16[128,1536]{1,0:T(8,128)(2,1)S(1)}, bf16[128,1536]{1,0:T(8,128)(2,1)S(1)}, u32[]{:S(2)}, u32[]{:S(2)}) collective-permute-start(bf16[128,1536]{1,0:T(8,128)(2,1)S(1)} %fusion.43), channel_id=1, source_target_pairs={{0,1},{1,0},{2,3},{3,2},{4,5},{5,4},{6,7},{7,6},{8,9},{9,8},{10,11... | collective-permute-start | bytes 1179656 | tf_op jit(solution)/shard_map/ppermute | solution.py:52
  36.7 1.7 collective-permute-start.2
  93.5 2.6 collective-permute-start.4
  95.5 2.2 collective-permute-start.6
  96.2 11.1 %collective-permute-start.5 = (bf16[128,1536]{1,0:T(8,128)(2,1)S(1)}, bf16[128,1536]{1,0:T(8,128)(2,1)S(1)}, u32[]{:S(2)}, u32[]{:S(2)}) collective-permute-start(bf16[128,1536]{1,0:T(8,128)(2,1)S(1)} %fusion.68), channel_id=1, source_target_pairs={{0,2},{2,0},{1,3},{3,1},{4,6},{6,4},{5,7},{7,5},{8,10},{10,8},{9,1... | collective-permute-start | bytes 1179656 | tf_op jit(solution)/shard_map/ppermute | solution.py:52
  108.1 12.1 %collective-permute-start.8 = (bf16[128,1536]{1,0:T(8,128)(2,1)S(1)}, bf16[128,1536]{1,0:T(8,128)(2,1)S(1)}, u32[]{:S(2)}, u32[]{:S(2)}) collective-permute-start(bf16[128,1536]{1,0:T(8,128)(2,1)S(1)} %add_convert_fusion), channel_id=1, source_target_pairs={{0,2},{2,0},{1,3},{3,1},{4,6},{6,4},{5,7},{7,5},{8,10},{10,8},{9,1... | collective-permute-start | bytes 1179656 | tf_op jit(solution)/shard_map/ppermute | solution.py:52
  109.7 17.3 %collective-permute-start.14 = (bf16[128,1536]{1,0:T(8,128)(2,1)S(1)}, bf16[128,1536]{1,0:T(8,128)(2,1)}, u32[]{:S(2)}, u32[]{:S(2)}) collective-permute-start(bf16[128,1536]{1,0:T(8,128)(2,1)S(1)} %fusion.50), channel_id=1, source_target_pairs={{0,2},{2,0},{1,3},{3,1},{4,6},{6,4},{5,7},{7,5},{8,10},{10,8},{9,1... | collective-permute-start | bytes 1179656 | tf_op jit(solution)/shard_map/ppermute | solution.py:52
  110.4 16.8 %collective-permute-start.7 = (bf16[128,1536]{1,0:T(8,128)(2,1)S(1)}, bf16[128,1536]{1,0:T(8,128)(2,1)S(1)}, u32[]{:S(2)}, u32[]{:S(2)}) collective-permute-start(bf16[128,1536]{1,0:T(8,128)(2,1)S(1)} %add_convert_fusion), channel_id=1, source_target_pairs={{0,1},{1,0},{2,3},{3,2},{4,5},{5,4},{6,7},{7,6},{8,9},{9,8},{10,11... | collective-permute-start | bytes 1179656 | tf_op jit(solution)/shard_map/ppermute | solution.py:52
  120.2 7.8 %collective-permute-start.9 = (bf16[128,1536]{1,0:T(8,128)(2,1)S(1)}, bf16[128,1536]{1,0:T(8,128)(2,1)}, u32[]{:S(2)}, u32[]{:S(2)}) collective-permute-start(bf16[128,1536]{1,0:T(8,128)(2,1)S(1)} %collective-permute-done.8), channel_id=1, source_target_pairs={{0,1},{1,0},{2,3},{3,2},{4,5},{5,4},{6,7},{7,6},{8,9},{9,8},{10,11... | collective-permute-start | bytes 1179656 | tf_op jit(solution)/shard_map/ppermute | solution.py:52
  120.2 45.1 %collective-permute-start.13 = (bf16[128,1536]{1,0:T(8,128)(2,1)S(1)}, bf16[128,1536]{1,0:T(8,128)(2,1)}, u32[]{:S(2)}, u32[]{:S(2)}) collective-permute-start(bf16[128,1536]{1,0:T(8,128)(2,1)S(1)} %fusion.50), channel_id=1, source_target_pairs={{0,1},{1,0},{2,3},{3,2},{4,5},{5,4},{6,7},{7,6},{8,9},{9,8},{10,11... | collective-permute-start | bytes 1179656 | tf_op jit(solution)/shard_map/ppermute | solution.py:52
  127.0 38.3 %collective-permute-start.15 = (bf16[128,1536]{1,0:T(8,128)(2,1)}, bf16[128,1536]{1,0:T(8,128)(2,1)}, u32[]{:S(2)}, u32[]{:S(2)}) collective-permute-start(bf16[128,1536]{1,0:T(8,128)(2,1)} %collective-permute-done.14), channel_id=1, source_target_pairs={{0,1},{1,0},{2,3},{3,2},{4,5},{5,4},{6,7},{7,6},{8,9},{9,8},{10,11... | collective-permute-start | bytes 1179656 | tf_op jit(solution)/shard_map/ppermute | solution.py:52
  172.7 9.2 %collective-permute-start.18 = (bf16[128,1536]{1,0:T(8,128)(2,1)S(1)}, bf16[128,1536]{1,0:T(8,128)(2,1)S(1)}, u32[]{:S(2)}, u32[]{:S(2)}) collective-permute-start(bf16[128,1536]{1,0:T(8,128)(2,1)S(1)} %slice.333), channel_id=1, source_target_pairs={{0,1},{1,0},{2,3},{3,2},{4,5},{5,4},{6,7},{7,6},{8,9},{9,8},{10,11... | collective-permute-start | bytes 1179656 | tf_op jit(solution)/shard_map/ppermute | solution.py:52
  174.3 4.4 %collective-permute-start.16 = (bf16[128,1536]{1,0:T(8,128)(2,1)S(1)}, bf16[128,1536]{1,0:T(8,128)(2,1)S(1)}, u32[]{:S(2)}, u32[]{:S(2)}) collective-permute-start(bf16[128,1536]{1,0:T(8,128)(2,1)S(1)} %slice.334), channel_id=1, source_target_pairs={{0,1},{1,0},{2,3},{3,2},{4,5},{5,4},{6,7},{7,6},{8,9},{9,8},{10,11... | collective-permute-start | bytes 1179656 | tf_op jit(solution)/shard_map/ppermute | solution.py:52
  177.9 13.3 %collective-permute-start.12 = (bf16[128,1536]{1,0:T(8,128)(2,1)S(1)}, bf16[128,1536]{1,0:T(8,128)(2,1)S(1)}, u32[]{:S(2)}, u32[]{:S(2)}) collective-permute-start(bf16[128,1536]{1,0:T(8,128)(2,1)S(1)} %slice.335), channel_id=1, source_target_pairs={{0,1},{1,0},{2,3},{3,2},{4,5},{5,4},{6,7},{7,6},{8,9},{9,8},{10,11... | collective-permute-start | bytes 1179656 | tf_op jit(solution)/shard_map/ppermute | solution.py:52
  178.0 2.3 collective-permute-start.10
  178.8 12.1 %collective-permute-start.17 = (bf16[128,1536]{1,0:T(8,128)(2,1)S(1)}, bf16[128,1536]{1,0:T(8,128)(2,1)S(1)}, u32[]{:S(2)}, u32[]{:S(2)}) collective-permute-start(bf16[128,1536]{1,0:T(8,128)(2,1)S(1)} %fusion.57), channel_id=1, source_target_pairs={{0,2},{2,0},{1,3},{3,1},{4,6},{6,4},{5,7},{7,5},{8,10},{10,8},{9,1... | collective-permute-start | bytes 1179656 | tf_op jit(solution)/shard_map/ppermute | solution.py:52
  180.4 18.0 %collective-permute-start.11 = (bf16[128,1536]{1,0:T(8,128)(2,1)S(1)}, bf16[128,1536]{1,0:T(8,128)(2,1)S(1)}, u32[]{:S(2)}, u32[]{:S(2)}) collective-permute-start(bf16[128,1536]{1,0:T(8,128)(2,1)S(1)} %fusion.64), channel_id=1, source_target_pairs={{0,2},{2,0},{1,3},{3,1},{4,6},{6,4},{5,7},{7,5},{8,10},{10,8},{9,1... | collective-permute-start | bytes 1179656 | tf_op jit(solution)/shard_map/ppermute | solution.py:52
  199.7 10.3 %collective-permute-start.20 = (bf16[128,1536]{1,0:T(8,128)(2,1)S(1)}, bf16[128,1536]{1,0:T(8,128)(2,1)S(1)}, u32[]{:S(2)}, u32[]{:S(2)}) collective-permute-start(bf16[128,1536]{1,0:T(8,128)(2,1)S(1)} %get-tuple-element.35), channel_id=1, source_target_pairs={{0,2},{2,0},{1,3},{3,1},{4,6},{6,4},{5,7},{7,5},{8,10},{10,8},{9,1... | collective-permute-start | bytes 1179656 | tf_op jit(solution)/shard_map/ppermute | solution.py:52
  201.2 8.8 %collective-permute-start.19 = (bf16[128,1536]{1,0:T(8,128)(2,1)S(1)}, bf16[128,1536]{1,0:T(8,128)(2,1)S(1)}, u32[]{:S(2)}, u32[]{:S(2)}) collective-permute-start(bf16[128,1536]{1,0:T(8,128)(2,1)S(1)} %get-tuple-element.35), channel_id=1, source_target_pairs={{0,1},{1,0},{2,3},{3,2},{4,5},{5,4},{6,7},{7,6},{8,9},{9,8},{10,11... | collective-permute-start | bytes 1179656 | tf_op jit(solution)/shard_map/ppermute | solution.py:52
  210.0 1.7 collective-permute-start.21
  234.8 169.5 %reduce-scatter.9.cloned.1.call-start = ((), (), s32[]{:S(2)}) async-start(), calls=%async_computation.5 | async-start | bytes 10027008
  272.2 3.9 collective-permute-start.22
  275.7 2.1 collective-permute-start.24
  276.2 11.2 %collective-permute-start.23 = (bf16[128,1536]{1,0:T(8,128)(2,1)S(1)}, bf16[128,1536]{1,0:T(8,128)(2,1)S(1)}, u32[]{:S(2)}, u32[]{:S(2)}) collective-permute-start(bf16[128,1536]{1,0:T(8,128)(2,1)S(1)} %fusion.53), channel_id=1, source_target_pairs={{0,2},{2,0},{1,3},{3,1},{4,6},{6,4},{5,7},{7,5},{8,10},{10,8},{9,1... | collective-permute-start | bytes 1179656 | tf_op jit(solution)/shard_map/ppermute | solution.py:52
  315.9 94.3 %collective-permute-start.25 = (bf16[48,1536]{0,1:T(8,128)(2,1)}, bf16[48,1536]{0,1:T(8,128)(2,1)S(1)}, u32[]{:S(2)}, u32[]{:S(2)}) collective-permute-start(bf16[48,1536]{0,1:T(8,128)(2,1)} %broadcast_select_fusion.1), channel_id=1, source_target_pairs={{0,4},{4,0},{1,5},{5,1},{2,6},{6,2},{3,7},{7,3},{8,12},{12,8},{9,1... | collective-permute-start | bytes 442376 | tf_op jit(solution)/shard_map/ppermute | solution.py:52
  407.2 9.4 %collective-permute-start.26 = (bf16[48,3072]{1,0:T(8,128)(2,1)}, bf16[48,3072]{1,0:T(8,128)(2,1)S(1)}, u32[]{:S(2)}, u32[]{:S(2)}) collective-permute-start(bf16[48,3072]{1,0:T(8,128)(2,1)} %copy.24), channel_id=1, source_target_pairs={{0,4},{4,0},{1,5},{5,1},{2,6},{6,2},{3,7},{7,3},{8,12},{12,8},{9,1... | collective-permute-start | bytes 884744 | tf_op jit(solution)/shard_map/ppermute | solution.py:52
  (37 other events, 718.1 us)
Sparse Core Ops, SparseCore 0:
  25.1 56.2 all-gather.2
  84.1 75.2 all-gather.4
  234.9 78.7 reduce-scatter.6
  317.0 87.2 reduce-scatter.8
